TPU v7x, 32 devices: a whole 2x2x4 slice. The times are simulated.
32 devices in a mesh: ctx: 16 (over z, y, x), tp: 2 (over core).
Axes of the slice: x: 2, y: 2, z: 4, core: 2. Of those that a mesh axis runs over, the one named last changes fastest.
Arguments:
- byte_states: bfloat16 [4096, 1024], P('ctx'), may hold values from -12 to 12, as said below
- patch_of_byte: int32 [4096], P('ctx'), may hold values from 0 to 125, as said below
- patch_first: int32 [16], replicated, may hold values from 0 to 991, as said below
- moved: int32 [2, 16], replicated, may hold values from 0 to 32, as said below
- w_qkv: bfloat16 [3, 1024, 2048], P(None, None, 'tp'), may hold values from -0.25 to 0.25, as said below
- d_attn: bfloat16 [1024, 2048], P('ctx', 'tp'), may hold values from -6 to 6
Outputs:
- attn_out: bfloat16 [1024, 2048], P('ctx', 'tp')
- byte_grad: bfloat16 [4096, 1024], P('ctx', 'tp')
Inputs may be any that keep to these rules, and one draw needn't show every extreme that they name: `patch_of_byte`: within each byte shard the numbers start at 0 and rise by 0 or 1 from byte to byte; a shard holds at most 126 patches, reached on some shard. `patch_first`: the sum of the patch counts of all earlier byte shards; shard 0 starts at 0. moved[0, 0] = 0 and moved[1, 15] = 0; every other entry is 1 to 32; every patch shard thereby receives exactly 64 patches, and the patch counts agree with patch_first and patch_of_byte. `w_qkv`: independent entries of order 1024 ** -0.5. `byte_states`: entries of order one.
All inputs are finite; a program needn't handle non-finite values.
Results may differ from a plain program's by a relative error of at most 0.011.
Values may be sent and summed in bfloat16 or wider, within the bound.
A program may use at most 64 MiB of HBM per device.

v0:
```python
import jax
import jax.numpy as jnp
from jax import lax
from jax.sharding import PartitionSpec as P

HD = 128


def extended_2(x, sides, width):
    for axis, dim in sides:
        peers, length = (lax.axis_size(axis), x.shape[dim])
        up = [(i, (i + 1) % peers) for i in range(peers - 1)]
        down = [(j, i) for i, j in up]
        last = lax.slice_in_dim(x, length - width, length, axis=dim)
        first = lax.slice_in_dim(x, 0, width, axis=dim)
        before = lax.ppermute(last, axis, up)
        after = lax.ppermute(first, axis, down)
        x = jnp.concatenate([before, x, after], axis=dim)
    return x


def pick_own(values, index):
    return lax.dynamic_index_in_dim(values, index, 0, keepdims=False)


def shards(byte_states, patch_of_byte, patch_first, moved, w_qkv, d_attn):
    ctx_index = lax.axis_index("ctx")
    n_ctx = lax.axis_size("ctx")
    rows = d_attn.shape[0]
    feats = d_attn.shape[1]
    heads = feats // HD
    capacity = 2 * rows
    total = rows * n_ctx
    scale = HD ** (-0.5)
    ends = jnp.concatenate([patch_first[1:], jnp.full((1,), total, jnp.int32)])
    counts = ends - patch_first
    lower_moves = moved[0]
    upper_moves = moved[1]
    zero_one = jnp.zeros((1,), jnp.int32)
    below_high = jnp.concatenate([zero_one, upper_moves[:-1]])
    above_low = jnp.concatenate([lower_moves[1:], zero_one])
    prev_first = jnp.concatenate([zero_one, patch_first[:-1]])
    prev_count = jnp.concatenate([zero_one, counts[:-1]])
    ranks = jnp.arange(rows, dtype=jnp.int32)[None, :]
    from_low = ranks < below_high[:, None]
    from_high = ranks >= (rows - above_low)[:, None]
    lower_local = prev_count[:, None] - below_high[:, None] + ranks
    own_local = lower_moves[:, None] + ranks - below_high[:, None]
    upper_local = ranks - (rows - above_low)[:, None]
    ids_all = jnp.where(
        from_low,
        prev_first[:, None] + lower_local,
        jnp.where(from_high, ends[:, None] + upper_local, patch_first[:, None] + own_local),
    )
    source_all = jnp.where(
        from_low,
        lower_local,
        jnp.where(from_high, 2 * capacity + upper_local, capacity + own_local),
    )
    wanted = pick_own(ids_all, ctx_index)
    source_rows = pick_own(source_all, ctx_index)
    key_place = ids_all.reshape(-1)
    slots = jnp.arange(capacity, dtype=jnp.int32)
    member = patch_of_byte[None, :] == slots[:, None]
    lengths = jnp.sum(member.astype(jnp.float32), axis=1)
    onehot = member.astype(jnp.bfloat16)
    part = byte_states.shape[1] // lax.axis_size("tp")
    source = lax.dynamic_slice_in_dim(byte_states, lax.axis_index("tp") * part, part, 1)
    pooled_local = (
        jnp.dot(onehot, source, preferred_element_type=jnp.float32)
        / jnp.maximum(lengths, 1.0)[:, None]
    ).astype(jnp.bfloat16)
    extended = extended_2(pooled_local, (("ctx", 0),), capacity)
    picker = (source_rows[:, None] == jnp.arange(3 * capacity, dtype=jnp.int32)[None, :]).astype(
        jnp.bfloat16
    )
    pooled = jnp.dot(picker, extended, preferred_element_type=jnp.float32).astype(jnp.bfloat16)
    pooled = lax.all_gather(pooled, "tp", axis=1, tiled=True)
    query = jnp.dot(pooled, w_qkv[0], preferred_element_type=jnp.float32).astype(jnp.bfloat16)
    keyed = jnp.dot(pooled, w_qkv[1], preferred_element_type=jnp.float32).astype(jnp.bfloat16)
    valued = jnp.dot(pooled, w_qkv[2], preferred_element_type=jnp.float32).astype(jnp.bfloat16)
    keys_all, values_all = (
        lax.all_gather(keyed, "ctx", axis=0, tiled=True),
        lax.all_gather(valued, "ctx", axis=0, tiled=True),
    )
    query3 = query.reshape(rows, heads, HD)
    keys3 = keys_all.reshape(total, heads, HD)
    values3 = values_all.reshape(total, heads, HD)
    causal = (wanted[:, None] >= key_place[None, :])[None, :, :]
    score = jnp.einsum("qhd,khd->hqk", query3, keys3, preferred_element_type=jnp.float32) * scale
    masked = jnp.where(causal, score, -jnp.inf)
    top = jnp.max(masked, axis=2, keepdims=True)
    lse = top + jnp.log(jnp.sum(jnp.exp(masked - top), axis=2, keepdims=True))
    prob = jnp.exp(jnp.where(causal, score - lse, -jnp.inf))
    probs = prob.astype(jnp.bfloat16)
    output3 = jnp.einsum("hqk,khd->qhd", probs, values3, preferred_element_type=jnp.float32).astype(
        jnp.bfloat16
    )
    attn_out = output3.reshape(rows, feats)
    grad3 = d_attn.reshape(rows, heads, HD)
    delta = jnp.sum(grad3.astype(jnp.float32) * output3.astype(jnp.float32), axis=2)
    dprob = jnp.einsum("qhd,khd->hqk", grad3, values3, preferred_element_type=jnp.float32)
    dscore = (prob * (dprob - jnp.transpose(delta)[:, :, None])).astype(jnp.bfloat16)
    d_query = (
        jnp.einsum("hqk,khd->qhd", dscore, keys3, preferred_element_type=jnp.float32) * scale
    ).astype(jnp.bfloat16)
    lse_rows = jnp.transpose(lse[:, :, 0])
    lse_all, delta_all = (
        lax.all_gather(lse_rows, "ctx", axis=0, tiled=True),
        lax.all_gather(delta, "ctx", axis=0, tiled=True),
    )
    own_keys = keyed.reshape(rows, heads, HD)
    own_values = valued.reshape(rows, heads, HD)
    q_piece = lax.all_gather(query, "ctx", axis=0, tiled=True)
    g_piece = lax.all_gather(d_attn, "ctx", axis=0, tiled=True)
    count = q_piece.shape[0]
    q_three = q_piece.reshape(count, heads, HD)
    g_three = g_piece.reshape(count, heads, HD)
    lse_piece = jnp.transpose(lse_all)
    delta_piece = jnp.transpose(delta_all)
    allowed = (key_place[:, None] >= wanted[None, :])[None, :, :]
    part_score = (
        jnp.einsum("qhd,khd->hqk", q_three, own_keys, preferred_element_type=jnp.float32) * scale
    )
    part_prob = jnp.exp(jnp.where(allowed, part_score - lse_piece[:, :, None], -jnp.inf))
    part_probs = part_prob.astype(jnp.bfloat16)
    d_value_sum = jnp.einsum(
        "hqk,qhd->khd", part_probs, g_three, preferred_element_type=jnp.float32
    )
    part_dprob = jnp.einsum("qhd,khd->hqk", g_three, own_values, preferred_element_type=jnp.float32)
    part_dscore = (part_prob * (part_dprob - delta_piece[:, :, None])).astype(jnp.bfloat16)
    d_key_sum = (
        jnp.einsum("hqk,qhd->khd", part_dscore, q_three, preferred_element_type=jnp.float32) * scale
    )
    d_key_sum, d_value_sum = (d_key_sum, d_value_sum)
    d_key = d_key_sum.astype(jnp.bfloat16).reshape(rows, feats)
    d_value = d_value_sum.astype(jnp.bfloat16).reshape(rows, feats)
    d_query = d_query.reshape(rows, feats)
    contract = (((1,), (1,)), ((), ()))
    partial_value = lax.dot_general(d_query, w_qkv[0], contract, preferred_element_type=jnp.float32)
    partial_value = partial_value + lax.dot_general(
        d_key, w_qkv[1], contract, preferred_element_type=jnp.float32
    )
    partial_value = partial_value + lax.dot_general(
        d_value, w_qkv[2], contract, preferred_element_type=jnp.float32
    )
    d_pooled = lax.psum_scatter(partial_value, "tp", scatter_dimension=1, tiled=True).astype(
        jnp.bfloat16
    )
    returned = extended_2(d_pooled, (("ctx", 0),), rows)
    my_count = pick_own(counts, ctx_index)
    my_low = pick_own(lower_moves, ctx_index)
    my_high = pick_own(upper_moves, ctx_index)
    my_below = pick_own(below_high, ctx_index)
    target = jnp.where(
        patch_of_byte < my_low,
        rows - my_low + patch_of_byte,
        jnp.where(
            patch_of_byte >= my_count - my_high,
            2 * rows + patch_of_byte - (my_count - my_high),
            rows + my_below + patch_of_byte - my_low,
        ),
    )
    chooser = (target[:, None] == jnp.arange(3 * rows, dtype=jnp.int32)[None, :]).astype(
        jnp.bfloat16
    )
    spread_back = jnp.dot(chooser, returned, preferred_element_type=jnp.float32)
    byte_lengths = jnp.sum(jnp.where(member, lengths[:, None], 0.0), axis=0)
    byte_grad = (spread_back / byte_lengths[:, None]).astype(jnp.bfloat16)
    return (attn_out, byte_grad)


def solution(mesh):
    placed = (P("ctx", None), P("ctx"), P(), P(), P(None, None, "tp"), P("ctx", "tp"))
    return jax.shard_map(
        shards,
        mesh=mesh,
        in_specs=placed,
        out_specs=(P("ctx", "tp"), P("ctx", "tp")),
        check_vma=False,
    )
```

profile of v0, /device:TPU:6, one launch (start us, length us, event | category | flops | bytes accessed | tf_op | source)
XLA Modules:
  0.0 305.7 jit_solution(10949627991634043434)
XLA Ops:
  7.2 0.7 all-gather.13.cloned.1.call-update
  8.0 0.8 convert_reduce_fusion
  8.8 0.9 fusion.56
  9.7 3.4 %collective-permute-start = (bf16[128,512]{1,0:T(8,128)(2,1)S(1)}, bf16[128,512]{1,0:T(8,128)(2,1)S(1)}, u32[]{:S(2)}, u32[]{:S(2)}) collective-permute-start(bf16[128,512]{1,0:T(8,128)(2,1)S(1)} %fusion.56), channel_id=1, source_target_pairs={{0,2},{2,4},{4,6},{6,8},{8,10},{10,12},{12,14},{14,16},{16,18},{18... | collective-permute-start | bytes 393224 | tf_op jit(solution)/shard_map/ppermute | solution.py:16
  13.1 2.4 collective-permute-start.1
  15.5 0.8 slice_bitcast_fusion.1
  16.4 0.8 fusion.133
  17.2 0.7 pad_add_fusion.3
  18.0 0.8 fusion.132
  19.2 1.2 dynamic-slice.3
  20.4 0.6 dynamic-slice.4
  21.0 0.6 dynamic-slice.2
  21.6 1.9 select_bitcast_fusion
  23.5 0.2 convolution_convert_fusion.1
  23.8 1.9 all_gather.21
  25.7 2.7 fusion.66
  28.5 2.7 fusion.60
  31.3 2.7 fusion.63
  35.4 36.0 %all-gather.13.cloned.1.call-done = bf16[1024,1024]{1,0:T(8,128)(2,1)} async-done(((bf16[64,1024]{1,0:T(8,128)(2,1)}), bf16[1024,1024]{1,0:T(8,128)(2,1)}) %all-gather.13.cloned.1.call-update) | async-done | bytes 2097168 | tf_op jit(solution)/shard_map/all_gather | solution.py:115
  71.4 2.9 copy.61
  74.3 59.7 %all-gather.9.cloned.1.call-done = bf16[1024,1024]{1,0:T(8,128)(2,1)} async-done(((bf16[64,1024]{1,0:T(8,128)(2,1)}), bf16[1024,1024]{1,0:T(8,128)(2,1)}) %all-gather.9.cloned.1.call-update) | async-done | bytes 2097168 | tf_op jit(solution)/shard_map/all_gather | solution.py:83
  134.0 2.6 select_reduce_fusion
  136.6 1.3 copy-done.2
  137.9 0.6 exponential_reduce_fusion
  138.5 33.8 %all-gather = f32[16,64,8]{1,2,0:T(8,128)S(1)} all-gather(f32[1,64,8]{1,2,0:T(8,128)S(1)} %bitcast.202), channel_id=1, replica_groups=mesh['ctx'=16,'tp'=2] {'ctx'}, dimensions={0}, use_global_device_ids=true | all-gather | bytes 34816 | tf_op jit(solution)/shard_map/all_gather | solution.py:109
  172.4 23.7 %all-gather.7.cloned.1.call-done = bf16[1024,1024]{1,0:T(8,128)(2,1)} async-done(((bf16[64,1024]{1,0:T(8,128)(2,1)}), bf16[1024,1024]{1,0:T(8,128)(2,1)}) %all-gather.7.cloned.1.call-update) | async-done | bytes 2097168 | tf_op jit(solution)/shard_map/all_gather | solution.py:84
  196.2 3.8 %multiply_reduce_fusion = (f32[64,8]{0,1:T(8,128)S(1)}, bf16[8,128,64]{1,2,0:T(8,128)(2,1)}) fusion(f32[8,64,1024]{2,1,0:T(8,128)} %copy-done.2, f32[8,64]{1,0:T(8,128)S(1)} %log_add_fusion, pred[64,1024]{1,0:T(8,128)(4,1)S(1)} %broadcast_compare_fusion.1, bf16[1024,1024]{1,0:T(8,128)(2,1)} %all-gather.7.cloned.1.call-done, bf16[64,1024]{1,0:T(8,128)(2,1)S(1)} %copy-done.6), kind=kOutput, calls=%fused_computation.75 | convolution fusion | flops 136642048 | bytes 4526080 | tf_op jit(solution)/shard_map/hqk,khd->qhd/dot_general | solution.py:96
  200.0 33.9 %all-gather.1 = f32[16,64,8]{1,2,0:T(8,128)S(1)} all-gather(f32[1,64,8]{1,2,0:T(8,128)S(1)} %bitcast.203), channel_id=1, replica_groups=mesh['ctx'=16,'tp'=2] {'ctx'}, dimensions={0}, use_global_device_ids=true | all-gather | bytes 34816 | tf_op jit(solution)/shard_map/all_gather | solution.py:110
  233.9 24.8 %all-gather.11.cloned.1.call-done = bf16[1024,1024]{1,0:T(8,128)(2,1)} async-done(((bf16[64,1024]{1,0:T(8,128)(2,1)}), bf16[1024,1024]{1,0:T(8,128)(2,1)}) %all-gather.11.cloned.1.call-update) | async-done | bytes 2097168 | tf_op jit(solution)/shard_map/all_gather | solution.py:114
  258.7 2.7 select_exponential_fusion
  261.4 0.9 fusion.78
  262.3 0.5 copy-done.1
  262.8 3.3 %fusion.75 = bf16[8,8,8,128]{3,2,1,0:T(8,128)(2,1)S(1)} fusion(f32[8,1024,64]{1,2,0:T(8,128)} %copy-done.1, bf16[1024,8,128]{0,2,1:T(8,128)(2,1)S(1)} %bitcast.199, f32[8,1024]{1,0:T(8,128)S(1)} %bitcast.200, bf16[1024,1024]{1,0:T(8,128)(2,1)} %all-gather.11.cloned.1.call-done, bf16[64,1024]{1,0:T(8,128)(2,1)S(1)} %copy-done.4), kind=kOutput, calls=%fused_computation.60 | convolution fusion | flops 270139392 | bytes 6586368 | tf_op jit(solution)/shard_map/hqk,qhd->khd/dot_general | solution.py:133
  266.1 2.5 fusion.14
  268.6 4.0 %fusion.79 = bf16[8,8,8,128]{3,2,1,0:T(8,128)(2,1)S(1)} fusion(f32[8,64,1024]{2,1,0:T(8,128)S(1)} %copy-done.3, f32[8,64]{1,0:T(8,128)S(1)} %bitcast.204, f32[8,64]{1,0:T(8,128)S(1)} %log_add_fusion, pred[64,1024]{1,0:T(8,128)(4,1)S(1)} %broadcast_compare_fusion.1, bf16[1024,1024]{1,0:T(8,128)(2,1)} %all-gather.7.cloned.1.call-done, ...), kind=kOutput, calls=%fused_computation.62 | convolution fusion | flops 271712256 | bytes 6623232 | tf_op jit(solution)/shard_map/hqk,khd->qhd/dot_general | solution.py:105
  272.6 2.4 fusion.47
  275.0 3.1 %fusion.44 = f32[64,1024]{1,0:T(8,128)} fusion(f32[64,1024]{1,0:T(8,128)S(1)} %fusion.47, bf16[3,1024,1024]{2,1,0:T(8,128)(2,1)} %param.10, bf16[8,8,8,128]{3,2,1,0:T(8,128)(2,1)S(1)} %fusion.78), kind=kOutput, calls=%fused_computation.47 | convolution fusion | flops 134283264 | bytes 2752512 | tf_op jit(solution)/shard_map/dot_general | solution.py:144
  278.1 0.6 dynamic_slice.27
  278.7 0.6 dynamic_slice.29
  279.3 0.7 constant_dynamic-slice_fusion.3
  282.7 0.7 compare_select_fusion.1
  283.4 2.6 reduce-scatter.2.cloned.1.call-done
  285.9 0.9 convert_element_type.89
  286.9 3.4 %collective-permute-start.2 = (bf16[64,512]{1,0:T(8,128)(2,1)S(1)}, bf16[64,512]{1,0:T(8,128)(2,1)S(1)}, u32[]{:S(2)}, u32[]{:S(2)}) collective-permute-start(bf16[64,512]{1,0:T(8,128)(2,1)S(1)} %convert_element_type.89), channel_id=1, source_target_pairs={{0,2},{2,4},{4,6},{6,8},{8,10},{10,12},{12,14},{14,16},{16,18},{18... | collective-permute-start | bytes 196616 | tf_op jit(solution)/shard_map/ppermute | solution.py:16
  290.2 2.5 collective-permute-start.3
  292.7 0.7 copy_bitcast_fusion
  293.4 4.8 %collective-permute-done.3 = bf16[64,512]{1,0:T(8,128)(2,1)S(1)} collective-permute-done((bf16[64,512]{1,0:T(8,128)(2,1)S(1)}, bf16[64,512]{1,0:T(8,128)(2,1)S(1)}, u32[]{:S(2)}, u32[]{:S(2)}) %collective-permute-start.3) | collective-permute-done | bytes 65568 | tf_op jit(solution)/shard_map/ppermute | solution.py:17
  298.2 1.0 fusion.43
  (65 shorter events, 2.5 us)
Async XLA Ops:
  7.2 1.6 copy-start
  7.2 64.3 %all-gather.13.cloned.1.call-start = ((), (), s32[]{:S(2)}) async-start(), calls=%async_computation.4 | async-start | bytes 2228224 | tf_op jit(solution)/shard_map/all_gather | solution.py:115
  7.9 126.1 %all-gather.9.cloned.1.call-start = ((), (), s32[]{:S(2)}) async-start(), calls=%async_computation.2 | async-start | bytes 2228224 | tf_op jit(solution)/shard_map/all_gather | solution.py:83
  9.7 13.9 %collective-permute-start = (bf16[128,512]{1,0:T(8,128)(2,1)S(1)}, bf16[128,512]{1,0:T(8,128)(2,1)S(1)}, u32[]{:S(2)}, u32[]{:S(2)}) collective-permute-start(bf16[128,512]{1,0:T(8,128)(2,1)S(1)} %fusion.56), channel_id=1, source_target_pairs={{0,2},{2,4},{4,6},{6,8},{8,10},{10,12},{12,14},{14,16},{16,18},{18... | collective-permute-start | bytes 393224 | tf_op jit(solution)/shard_map/ppermute | solution.py:16
  13.1 10.5 %collective-permute-start.1 = (bf16[128,512]{1,0:T(8,128)(2,1)S(1)}, bf16[128,512]{1,0:T(8,128)(2,1)S(1)}, u32[]{:S(2)}, u32[]{:S(2)}) collective-permute-start(bf16[128,512]{1,0:T(8,128)(2,1)S(1)} %fusion.56), channel_id=1, source_target_pairs={{2,0},{4,2},{6,4},{8,6},{10,8},{12,10},{14,12},{16,14},{18,16},{20... | collective-permute-start | bytes 393224 | tf_op jit(solution)/shard_map/ppermute | solution.py:17
  28.4 167.7 %all-gather.7.cloned.1.call-start = ((), (), s32[]{:S(2)}) async-start(), calls=%async_computation.1 | async-start | bytes 2228224 | tf_op jit(solution)/shard_map/all_gather | solution.py:84
  31.2 3.7 %copy-start.9 = (s32[16]{0:T(128)S(1)}, s32[16]{0:T(128)}, u32[]{:S(2)}) copy-start(s32[16]{0:T(128)} %param.8) | copy-start | bytes 196
  31.2 227.5 %all-gather.11.cloned.1.call-start = ((), (), s32[]{:S(2)}) async-start(), calls=%async_computation.3 | async-start | bytes 2228224 | tf_op jit(solution)/shard_map/all_gather | solution.py:114
  34.0 251.9 %reduce-scatter.2.cloned.1.call-start = ((), (), s32[]{:S(2)}) async-start(), calls=%async_computation.5 | async-start | bytes 393216 | tf_op jit(solution)/shard_map/reduce_scatter | solution.py:147
  35.4 98.6 %copy-start.5 = (bf16[64,1024]{1,0:T(8,128)(2,1)S(1)}, bf16[64,1024]{1,0:T(8,128)(2,1)}, u32[]{:S(2)}) copy-start(bf16[64,1024]{1,0:T(8,128)(2,1)} %fusion.63) | copy-start | bytes 393220
  136.6 1.4 copy-start.2
  136.6 59.6 %copy-start.6 = (bf16[64,1024]{1,0:T(8,128)(2,1)S(1)}, bf16[64,1024]{1,0:T(8,128)(2,1)}, u32[]{:S(2)}) copy-start(bf16[64,1024]{1,0:T(8,128)(2,1)} %param.11) | copy-start | bytes 393220
  172.4 86.3 %copy-start.7 = (bf16[64,1024]{1,0:T(8,128)(2,1)S(1)}, bf16[64,1024]{1,0:T(8,128)(2,1)}, u32[]{:S(2)}) copy-start(bf16[64,1024]{1,0:T(8,128)(2,1)} %fusion.66) | copy-start | bytes 393220
  261.4 1.4 copy-start.1
  261.4 1.4 copy-start.4
  266.1 2.5 copy-start.3
  275.0 7.6 %copy-start.10 = (s32[256]{0:T(256)S(1)}, s32[256]{0:T(256)}, u32[]{:S(2)}) copy-start(s32[256]{0:T(256)} %param.7) | copy-start | bytes 3076
  275.0 17.7 %copy-start.8 = (bf16[8,128,64]{1,2,0:T(8,128)(2,1)S(1)}, bf16[8,128,64]{1,2,0:T(8,128)(2,1)}, u32[]{:S(2)}) copy-start(bf16[8,128,64]{1,2,0:T(8,128)(2,1)} %get-tuple-element.18) | copy-start | bytes 393220
  286.9 6.5 %collective-permute-start.2 = (bf16[64,512]{1,0:T(8,128)(2,1)S(1)}, bf16[64,512]{1,0:T(8,128)(2,1)S(1)}, u32[]{:S(2)}, u32[]{:S(2)}) collective-permute-start(bf16[64,512]{1,0:T(8,128)(2,1)S(1)} %convert_element_type.89), channel_id=1, source_target_pairs={{0,2},{2,4},{4,6},{6,8},{8,10},{10,12},{12,14},{14,16},{16,18},{18... | collective-permute-start | bytes 196616 | tf_op jit(solution)/shard_map/ppermute | solution.py:16
  290.2 8.0 %collective-permute-start.3 = (bf16[64,512]{1,0:T(8,128)(2,1)S(1)}, bf16[64,512]{1,0:T(8,128)(2,1)S(1)}, u32[]{:S(2)}, u32[]{:S(2)}) collective-permute-start(bf16[64,512]{1,0:T(8,128)(2,1)S(1)} %convert_element_type.89), channel_id=1, source_target_pairs={{2,0},{4,2},{6,4},{8,6},{10,8},{12,10},{14,12},{16,14},{18,16},{20... | collective-permute-start | bytes 196616 | tf_op jit(solution)/shard_map/ppermute | solution.py:17
Sparse Core Ops, SparseCore 0:
  10.8 60.6 all-gather.12
  74.8 59.1 all-gather.8
  136.8 59.3 all-gather.6
  199.4 59.2 all-gather.10
  278.3 7.6 reduce-scatter.1
where the time goes:
time: 306 us
  waiting for transfers between devices  152 us (50%)
  blocking collectives  69.5 us (23%)
  matrix products  35.5 us (12%)
  between operations  16.7 us (5%)
  local copies, waits for them, and re-layouts  13.3 us (4%)
  starting transfers between devices  11.9 us (4%)
  other arithmetic  6.49 us (2%)
    all_gather x1, waiting for transfers between devices, shards(): lax.all_gather(keyed, 'ctx', axis=0, tiled=True)  59.7 us
    all_gather x1, waiting for transfers between devices, shards(): g_piece = lax.all_gather(d_attn, 'ctx', axis=0, tiled=True)  36 us
    all_gather x1, blocking collectives, shards(): lax.all_gather(delta, 'ctx', axis=0, tiled=True)  33.9 us
    all_gather x1, blocking collectives, shards(): lax.all_gather(lse_rows, 'ctx', axis=0, tiled=True)  33.8 us
    all_gather x1, waiting for transfers between devices, shards(): q_piece = lax.all_gather(query, 'ctx', axis=0, tiled=True)  24.8 us
    all_gather x1, waiting for transfers between devices, shards(): lax.all_gather(valued, 'ctx', axis=0, tiled=True)  23.7 us
    ppermute x2, starting transfers between devices, extended_2(): before = lax.ppermute(last, axis, up)  6.77 us
  transfers between devices with their start and end apart: 9, of which 6 were waited for; matrix products, arithmetic and copies ran while one was open for 11% of the time, Pallas kernels for 0%

commit v1 on v0

--- a/solution.py
+++ b/solution.py
@@ -79,9 +79,24 @@
     query = jnp.dot(pooled, w_qkv[0], preferred_element_type=jnp.float32).astype(jnp.bfloat16)
     keyed = jnp.dot(pooled, w_qkv[1], preferred_element_type=jnp.float32).astype(jnp.bfloat16)
     valued = jnp.dot(pooled, w_qkv[2], preferred_element_type=jnp.float32).astype(jnp.bfloat16)
+
+    def test_the_points(block_here):
+        chip_axis = "ctx"
+        latest, frame_out = (jax.lax.axis_size(chip_axis), jax.lax.axis_index(chip_axis))
+        a_now, part_now = (block_here, 1)
+        while part_now < latest:
+            high = jax.lax.ppermute(
+                a_now, axis_name=chip_axis, perm=[(kk, kk ^ part_now) for kk in range(latest)]
+            )
+            v_next = jnp.concatenate([a_now, high], axis=0)
+            upper = jnp.concatenate([high, a_now], axis=0)
+            a_now = jnp.where(frame_out & part_now == 0, v_next, upper)
+            part_now = 2 * part_now
+        return a_now
+
     keys_all, values_all = (
         lax.all_gather(keyed, "ctx", axis=0, tiled=True),
-        lax.all_gather(valued, "ctx", axis=0, tiled=True),
+        test_the_points(valued),
     )
     query3 = query.reshape(rows, heads, HD)
     keys3 = keys_all.reshape(total, heads, HD)

time: 306 us -> 295 us (0.964)
  waiting for transfers between devices: 152 us -> 124 us
  starting transfers between devices: 11.9 us -> 18.2 us
  blocking collectives: 69.5 us -> 75 us
    ppermute x0 -> x4, waiting for transfers between devices: none -> 75.2 us  [test_the_points(): jax.lax.ppermute(a_now, axis_name=chip_axis, perm=[(kk, kk ^ part_now) fo...]
    all_gather x1, waiting for transfers between devices: 36 us -> 0.01 us  [shards(): g_piece = lax.all_gather(d_attn, 'ctx', axis=0, tiled=True)]
    all_gather x1, waiting for transfers between devices: 24.8 us -> 0.01 us  [shards(): q_piece = lax.all_gather(query, 'ctx', axis=0, tiled=True)]
    all_gather x1 -> x0, waiting for transfers between devices: 23.7 us -> none  [shards(): lax.all_gather(valued, 'ctx', axis=0, tiled=True)]
    all_gather x1, waiting for transfers between devices: 59.7 us -> 39.4 us  [shards(): lax.all_gather(keyed, 'ctx', axis=0, tiled=True)]
    ppermute x0 -> x4, starting transfers between devices: none -> 6.37 us  [test_the_points(): jax.lax.ppermute(a_now, axis_name=chip_axis, perm=[(kk, kk ^ part_now) fo...]
    all_gather x1, blocking collectives: 33.9 us -> 39.4 us  [shards(): lax.all_gather(delta, 'ctx', axis=0, tiled=True)]
  transfers between devices with their start and end apart: 9 -> 12, of which waited for: 6 -> 7; matrix products, arithmetic and copies ran while one was open for 11% -> 12% of each run, Pallas kernels for 0% -> 0%
where the time goes in v1:
time: 295 us; the launch traced here: 294 us
  waiting for transfers between devices  124 us (42%)
  blocking collectives  75 us (25%)
  matrix products  36.8 us (12%)
  starting transfers between devices  18.2 us (6%)
  between operations  16.7 us (6%)
  local copies, waits for them, and re-layouts  14.8 us (5%)
  other arithmetic  8.51 us (3%)
    ppermute x4, waiting for transfers between devices, test_the_points(): jax.lax.ppermute(a_now, axis_name=chip_axis, perm=[(kk, kk ^ part_now) fo...  75.2 us
    all_gather x1, waiting for transfers between devices, shards(): lax.all_gather(keyed, 'ctx', axis=0, tiled=True)  39.4 us
    all_gather x1, blocking collectives, shards(): lax.all_gather(delta, 'ctx', axis=0, tiled=True)  39.4 us
    all_gather x1, blocking collectives, shards(): lax.all_gather(lse_rows, 'ctx', axis=0, tiled=True)  33.8 us
    ppermute x2, starting transfers between devices, extended_2(): before = lax.ppermute(last, axis, up)  6.78 us
    ppermute x4, starting transfers between devices, test_the_points(): jax.lax.ppermute(a_now, axis_name=chip_axis, perm=[(kk, kk ^ part_now) fo...  6.37 us
  transfers between devices with their start and end apart: 12, of which 7 were waited for; matrix products, arithmetic and copies ran while one was open for 12% of the time, Pallas kernels for 0%

profile of v1, /device:TPU:6, one launch (start us, length us, event | category | flops | bytes accessed | tf_op | source)
XLA Modules:
  0.0 294.1 jit_solution(3506044260968562523)
XLA Ops:
  7.2 0.7 all-gather.10.cloned.1.call-update
  8.0 0.8 convert_reduce_fusion
  8.8 0.9 fusion.48
  9.7 3.4 %collective-permute-start = (bf16[128,512]{1,0:T(8,128)(2,1)S(1)}, bf16[128,512]{1,0:T(8,128)(2,1)S(1)}, u32[]{:S(2)}, u32[]{:S(2)}) collective-permute-start(bf16[128,512]{1,0:T(8,128)(2,1)S(1)} %fusion.48), channel_id=1, source_target_pairs={{0,2},{2,4},{4,6},{6,8},{8,10},{10,12},{12,14},{14,16},{16,18},{18... | collective-permute-start | bytes 393224 | tf_op jit(solution)/shard_map/ppermute | solution.py:16
  13.1 2.4 collective-permute-start.1
  15.5 0.8 slice_bitcast_fusion.1
  16.4 0.8 fusion.119
  17.2 0.7 pad_add_fusion.3
  18.0 0.8 fusion.118
  19.2 1.2 dynamic-slice.3
  21.0 0.6 dynamic-slice.2
  21.6 1.9 select_bitcast_fusion
  23.8 1.9 all_gather.18
  25.7 2.7 fusion.58
  28.5 2.1 fusion.52
  30.6 1.5 collective-permute-start.2
  32.1 2.7 fusion.55
  34.9 1.3 collective-permute-done.2
  37.9 7.8 %collective-permute-done.3 = bf16[128,1024]{1,0:T(8,128)(2,1)S(1)} collective-permute-done((bf16[128,1024]{1,0:T(8,128)(2,1)S(1)}, bf16[128,1024]{1,0:T(8,128)(2,1)S(1)}, u32[]{:S(2)}, u32[]{:S(2)}) %collective-permute-start.3) | collective-permute-done | bytes 262176 | tf_op jit(solution)/shard_map/ppermute | solution.py:88
  45.9 1.6 collective-permute-start.4
  47.7 18.3 %collective-permute-done.4 = bf16[256,1024]{1,0:T(8,128)(2,1)S(1)} collective-permute-done((bf16[256,1024]{1,0:T(8,128)(2,1)S(1)}, bf16[256,1024]{1,0:T(8,128)(2,1)S(1)}, u32[]{:S(2)}, u32[]{:S(2)}) %collective-permute-start.4) | collective-permute-done | bytes 524320 | tf_op jit(solution)/shard_map/ppermute | solution.py:88
  66.5 2.7 collective-permute-start.5
  69.7 1.3 maximum_select_fusion.1
  71.0 47.8 %collective-permute-done.5 = bf16[512,1024]{1,0:T(8,128)(2,1)S(1)} collective-permute-done((bf16[512,1024]{1,0:T(8,128)(2,1)S(1)}, bf16[512,1024]{1,0:T(8,128)(2,1)S(1)}, u32[]{:S(2)}, u32[]{:S(2)}) %collective-permute-start.5) | collective-permute-done | bytes 1048608 | tf_op jit(solution)/shard_map/ppermute | solution.py:88
  118.8 1.2 copy_bitcast_fusion
  120.0 2.9 copy.95
  122.9 39.4 %all-gather.6.cloned.1.call-done = bf16[1024,1024]{1,0:T(8,128)(2,1)} async-done(((bf16[64,1024]{1,0:T(8,128)(2,1)}), bf16[1024,1024]{1,0:T(8,128)(2,1)}) %all-gather.6.cloned.1.call-update) | async-done | bytes 2097168 | tf_op jit(solution)/shard_map/all_gather | solution.py:98
  162.3 2.6 select_reduce_fusion
  164.9 1.3 copy-done.2
  166.8 33.8 %all-gather = f32[16,64,8]{1,2,0:T(8,128)S(1)} all-gather(f32[1,64,8]{1,2,0:T(8,128)S(1)} %bitcast.203), channel_id=1, replica_groups=mesh['ctx'=16,'tp'=2] {'ctx'}, dimensions={0}, use_global_device_ids=true | all-gather | bytes 34816 | tf_op jit(solution)/shard_map/all_gather | solution.py:124
  200.7 4.9 %multiply_reduce_fusion = (f32[64,8]{0,1:T(8,128)S(1)}, bf16[8,128,64]{1,2,0:T(8,128)(2,1)}) fusion(bf16[512,8,128]{2,0,1:T(8,128)(2,1)} %copy_bitcast_fusion, bf16[512,8,128]{2,0,1:T(8,128)(2,1)} %maximum_select_fusion.1, pred[]{:T(512)S(6)} %eq.53, f32[8,64,1024]{2,1,0:T(8,128)} %copy-done.2, f32[8,64]{1,0:T(8,128)S(1)} %log_add_fusion, ...), kind=kOutput, calls=%fused_computation.79 | convolution fusion | flops 146079232 | bytes 4526081 | tf_op jit(solution)/shard_map/hqk,khd->qhd/dot_general | solution.py:111
  205.6 39.4 %all-gather.1 = f32[16,64,8]{1,2,0:T(8,128)S(1)} all-gather(f32[1,64,8]{1,2,0:T(8,128)S(1)} %bitcast.204), channel_id=1, replica_groups=mesh['ctx'=16,'tp'=2] {'ctx'}, dimensions={0}, use_global_device_ids=true | all-gather | bytes 34816 | tf_op jit(solution)/shard_map/all_gather | solution.py:125
  245.1 2.7 select_exponential_fusion
  247.8 0.9 fusion.67
  249.2 3.3 %fusion.64 = bf16[8,8,8,128]{3,2,1,0:T(8,128)(2,1)S(1)} fusion(f32[8,1024,64]{1,2,0:T(8,128)} %copy-done.1, bf16[1024,8,128]{0,2,1:T(8,128)(2,1)S(1)} %bitcast.200, f32[8,1024]{1,0:T(8,128)S(1)} %bitcast.201, bf16[1024,1024]{1,0:T(8,128)(2,1)} %all-gather.8.cloned.1.call-done, bf16[64,1024]{1,0:T(8,128)(2,1)S(1)} %fusion.52), kind=kOutput, calls=%fused_computation.55 | convolution fusion | flops 270139392 | bytes 6586368 | tf_op jit(solution)/shard_map/hqk,qhd->khd/dot_general | solution.py:148
  252.6 2.5 fusion.10
  255.1 4.9 %fusion.68 = bf16[8,8,8,128]{3,2,1,0:T(8,128)(2,1)S(1)} fusion(f32[8,64,1024]{2,1,0:T(8,128)S(1)} %copy-done.3, f32[8,64]{1,0:T(8,128)S(1)} %bitcast.205, f32[8,64]{1,0:T(8,128)S(1)} %log_add_fusion, pred[64,1024]{1,0:T(8,128)(4,1)S(1)} %broadcast_compare_fusion.1, bf16[512,8,128]{2,0,1:T(8,128)(2,1)} %copy_bitcast_fusion, ...), kind=kOutput, calls=%fused_computation.57 | convolution fusion | flops 281149440 | bytes 6623233 | tf_op jit(solution)/shard_map/hqk,khd->qhd/dot_general | solution.py:120
  259.9 2.4 fusion.39
  262.3 3.1 %fusion.36 = f32[64,1024]{1,0:T(8,128)} fusion(f32[64,1024]{1,0:T(8,128)S(1)} %fusion.39, bf16[3,1024,1024]{2,1,0:T(8,128)(2,1)} %param.10, bf16[8,8,8,128]{3,2,1,0:T(8,128)(2,1)S(1)} %fusion.67), kind=kOutput, calls=%fused_computation.42 | convolution fusion | flops 134283264 | bytes 2752512 | tf_op jit(solution)/shard_map/dot_general | solution.py:159
  265.4 0.6 dynamic_slice.27
  266.6 0.7 constant_dynamic-slice_fusion.3
  270.5 3.8 %reduce-scatter.2.cloned.1.call-done = f32[64,512]{1,0:T(8,128)} async-done(((f32[64,1024]{1,0:T(8,128)}), f32[64,512]{1,0:T(8,128)}) %reduce-scatter.2.cloned.1.call-update) | async-done | bytes 131088 | tf_op jit(solution)/shard_map/reduce_scatter | solution.py:162
  274.3 0.9 convert_element_type.89
  275.3 3.4 %collective-permute-start.6 = (bf16[64,512]{1,0:T(8,128)(2,1)S(1)}, bf16[64,512]{1,0:T(8,128)(2,1)S(1)}, u32[]{:S(2)}, u32[]{:S(2)}) collective-permute-start(bf16[64,512]{1,0:T(8,128)(2,1)S(1)} %convert_element_type.89), channel_id=1, source_target_pairs={{0,2},{2,4},{4,6},{6,8},{8,10},{10,12},{12,14},{14,16},{16,18},{18... | collective-permute-start | bytes 196616 | tf_op jit(solution)/shard_map/ppermute | solution.py:16
  278.6 2.5 collective-permute-start.7
  281.1 0.7 copy_bitcast_fusion.3
  281.8 4.8 %collective-permute-done.7 = bf16[64,512]{1,0:T(8,128)(2,1)S(1)} collective-permute-done((bf16[64,512]{1,0:T(8,128)(2,1)S(1)}, bf16[64,512]{1,0:T(8,128)(2,1)S(1)}, u32[]{:S(2)}, u32[]{:S(2)}) %collective-permute-start.7) | collective-permute-done | bytes 65568 | tf_op jit(solution)/shard_map/ppermute | solution.py:17
  286.6 1.0 fusion.35
  (81 shorter events, 7.1 us)
Async XLA Ops:
  7.2 1.6 copy-start
  7.2 112.8 %all-gather.10.cloned.1.call-start = ((), (), s32[]{:S(2)}) async-start(), calls=%async_computation.3 | async-start | bytes 2228224 | tf_op jit(solution)/shard_map/all_gather | solution.py:130
  7.9 154.4 %all-gather.6.cloned.1.call-start = ((), (), s32[]{:S(2)}) async-start(), calls=%async_computation.1 | async-start | bytes 2228224 | tf_op jit(solution)/shard_map/all_gather | solution.py:98
  9.7 13.9 %collective-permute-start = (bf16[128,512]{1,0:T(8,128)(2,1)S(1)}, bf16[128,512]{1,0:T(8,128)(2,1)S(1)}, u32[]{:S(2)}, u32[]{:S(2)}) collective-permute-start(bf16[128,512]{1,0:T(8,128)(2,1)S(1)} %fusion.48), channel_id=1, source_target_pairs={{0,2},{2,4},{4,6},{6,8},{8,10},{10,12},{12,14},{14,16},{16,18},{18... | collective-permute-start | bytes 393224 | tf_op jit(solution)/shard_map/ppermute | solution.py:16
  13.1 10.5 %collective-permute-start.1 = (bf16[128,512]{1,0:T(8,128)(2,1)S(1)}, bf16[128,512]{1,0:T(8,128)(2,1)S(1)}, u32[]{:S(2)}, u32[]{:S(2)}) collective-permute-start(bf16[128,512]{1,0:T(8,128)(2,1)S(1)} %fusion.48), channel_id=1, source_target_pairs={{2,0},{4,2},{6,4},{8,6},{10,8},{12,10},{14,12},{16,14},{18,16},{20... | collective-permute-start | bytes 393224 | tf_op jit(solution)/shard_map/ppermute | solution.py:17
  28.5 216.7 %all-gather.8.cloned.1.call-start = ((), (), s32[]{:S(2)}) async-start(), calls=%async_computation.2 | async-start | bytes 2228224 | tf_op jit(solution)/shard_map/all_gather | solution.py:129
  30.6 7.1 %copy-start.9 = (s32[16]{0:T(128)S(1)}, s32[16]{0:T(128)}, u32[]{:S(2)}) copy-start(s32[16]{0:T(128)} %param.8) | copy-start | bytes 196
  30.6 5.6 %collective-permute-start.2 = (bf16[64,1024]{1,0:T(8,128)(2,1)S(1)}, bf16[64,1024]{1,0:T(8,128)(2,1)S(1)}, u32[]{:S(2)}, u32[]{:S(2)}) collective-permute-start(bf16[64,1024]{1,0:T(8,128)(2,1)S(1)} %fusion.52), channel_id=1, source_target_pairs={{0,2},{2,0},{4,6},{6,4},{8,10},{10,8},{12,14},{14,12},{16,18},{18,... | collective-permute-start | bytes 393224 | tf_op jit(solution)/shard_map/ppermute | solution.py:88
  34.8 239.5 %reduce-scatter.2.cloned.1.call-start = ((), (), s32[]{:S(2)}) async-start(), calls=%async_computation.4 | async-start | bytes 393216 | tf_op jit(solution)/shard_map/reduce_scatter | solution.py:162
  36.3 9.4 %collective-permute-start.3 = (bf16[128,1024]{1,0:T(8,128)(2,1)S(1)}, bf16[128,1024]{1,0:T(8,128)(2,1)S(1)}, u32[]{:S(2)}, u32[]{:S(2)}) collective-permute-start(bf16[128,1024]{1,0:T(8,128)(2,1)S(1)} %maximum_select_fusion.9), channel_id=1, source_target_pairs={{0,4},{2,6},{4,0},{6,2},{8,12},{10,14},{12,8},{14,10},{16,20},{18,... | collective-permute-start | bytes 786440 | tf_op jit(solution)/shard_map/ppermute | solution.py:88
  45.9 20.2 %collective-permute-start.4 = (bf16[256,1024]{1,0:T(8,128)(2,1)S(1)}, bf16[256,1024]{1,0:T(8,128)(2,1)S(1)}, u32[]{:S(2)}, u32[]{:S(2)}) collective-permute-start(bf16[256,1024]{1,0:T(8,128)(2,1)S(1)} %maximum_select_fusion.4), channel_id=1, source_target_pairs={{0,8},{2,10},{4,12},{6,14},{8,0},{10,2},{12,4},{14,6},{16,24},{18,... | collective-permute-start | bytes 1572872 | tf_op jit(solution)/shard_map/ppermute | solution.py:88
  66.5 52.2 %collective-permute-start.5 = (bf16[512,1024]{1,0:T(8,128)(2,1)S(1)}, bf16[512,1024]{1,0:T(8,128)(2,1)S(1)}, u32[]{:S(2)}, u32[]{:S(2)}) collective-permute-start(bf16[512,1024]{1,0:T(8,128)(2,1)S(1)} %maximum_select_fusion.2), channel_id=1, source_target_pairs={{0,16},{2,18},{4,20},{6,22},{8,24},{10,26},{12,28},{14,30},{16,0},... | collective-permute-start | bytes 3145736 | tf_op jit(solution)/shard_map/ppermute | solution.py:88
  120.0 42.3 %copy-start.4 = (bf16[64,1024]{1,0:T(8,128)(2,1)S(1)}, bf16[64,1024]{1,0:T(8,128)(2,1)}, u32[]{:S(2)}) copy-start(bf16[64,1024]{1,0:T(8,128)(2,1)} %fusion.55) | copy-start | bytes 393220
  164.9 1.3 copy-start.2
  164.9 35.8 %copy-start.5 = (bf16[64,1024]{1,0:T(8,128)(2,1)S(1)}, bf16[64,1024]{1,0:T(8,128)(2,1)}, u32[]{:S(2)}) copy-start(bf16[64,1024]{1,0:T(8,128)(2,1)} %param.11) | copy-start | bytes 393220
  200.7 44.4 %copy-start.7 = (bf16[64,1024]{1,0:T(8,128)(2,1)S(1)}, bf16[64,1024]{1,0:T(8,128)(2,1)}, u32[]{:S(2)}) copy-start(bf16[64,1024]{1,0:T(8,128)(2,1)} %fusion.58) | copy-start | bytes 393220
  247.8 1.4 copy-start.1
  252.5 2.5 copy-start.3
  252.5 2.5 copy-start.6
  262.3 7.5 %copy-start.10 = (s32[256]{0:T(256)S(1)}, s32[256]{0:T(256)}, u32[]{:S(2)}) copy-start(s32[256]{0:T(256)} %param.7) | copy-start | bytes 3076
  262.3 18.8 %copy-start.8 = (bf16[8,128,64]{1,2,0:T(8,128)(2,1)S(1)}, bf16[8,128,64]{1,2,0:T(8,128)(2,1)}, u32[]{:S(2)}) copy-start(bf16[8,128,64]{1,2,0:T(8,128)(2,1)} %get-tuple-element.18) | copy-start | bytes 393220
  275.3 6.5 %collective-permute-start.6 = (bf16[64,512]{1,0:T(8,128)(2,1)S(1)}, bf16[64,512]{1,0:T(8,128)(2,1)S(1)}, u32[]{:S(2)}, u32[]{:S(2)}) collective-permute-start(bf16[64,512]{1,0:T(8,128)(2,1)S(1)} %convert_element_type.89), channel_id=1, source_target_pairs={{0,2},{2,4},{4,6},{6,8},{8,10},{10,12},{12,14},{14,16},{16,18},{18... | collective-permute-start | bytes 196616 | tf_op jit(solution)/shard_map/ppermute | solution.py:16
  278.6 8.0 %collective-permute-start.7 = (bf16[64,512]{1,0:T(8,128)(2,1)S(1)}, bf16[64,512]{1,0:T(8,128)(2,1)S(1)}, u32[]{:S(2)}, u32[]{:S(2)}) collective-permute-start(bf16[64,512]{1,0:T(8,128)(2,1)S(1)} %convert_element_type.89), channel_id=1, source_target_pairs={{2,0},{4,2},{6,4},{8,6},{10,8},{12,10},{14,12},{16,14},{18,16},{20... | collective-permute-start | bytes 196616 | tf_op jit(solution)/shard_map/ppermute | solution.py:17
Sparse Core Ops, SparseCore 0:
  10.8 86.3 all-gather.9
  100.5 61.7 all-gather.5
  165.6 59.5 all-gather.7
  265.5 8.7 reduce-scatter.1
